TPU v7x, 32 devices: a 4x4x1 block of a 4x4x8 slice. The times are simulated.
32 devices in a mesh: dp: 1 (over z), tx: 4 (over y), ty: 8 (over x, core).
Axes of the slice: x: 4, y: 4, z: 1, core: 2. Of those that a mesh axis runs over, the one named last changes fastest.
The devices are a block of a 4x4x8 slice.
Arguments:
- x_in: bfloat16 [24, 576, 1024], P('dp', None, 'tx')
- ln1_gain: float32 [2, 1024], P(None, 'tx')
- ln1_bias: float32 [2, 1024], P(None, 'tx')
- w_q: bfloat16 [2, 1024, 16, 64], P(None, 'tx', 'ty')
- b_q: float32 [2, 16, 64], P(None, 'ty')
- w_k: bfloat16 [2, 1024, 16, 64], P(None, 'tx', 'ty')
- w_v: bfloat16 [2, 1024, 16, 64], P(None, 'tx', 'ty')
- b_v: float32 [2, 16, 64], P(None, 'ty')
- w_o: bfloat16 [2, 16, 64, 1024], P(None, 'ty', None, 'tx')
- b_o: float32 [2, 1024], P(None, 'tx')
- ln2_gain: float32 [2, 1024], P(None, 'tx')
- ln2_bias: float32 [2, 1024], P(None, 'tx')
- w_up: bfloat16 [2, 1024, 4096], P(None, 'tx', 'ty')
- b_up: float32 [2, 4096], P(None, 'ty')
- w_down: bfloat16 [2, 4096, 1024], P(None, 'ty', 'tx')
- b_down: float32 [2, 1024], P(None, 'tx')
Outputs:
- output: bfloat16 [24, 576, 1024], P('dp', None, 'tx')
All inputs are finite; a program needn't handle non-finite values.
Results may differ from a plain program's by a relative error of at most 0.02.
Values are sent between devices in bfloat16 or wider.
A program may use at most 768 MiB of HBM per device.

v0:
```python
import jax
import jax.numpy as jnp
from jax import lax
from jax.sharding import PartitionSpec as P

EPS = 1e-6


def split_norm(x_f, gain, shift, width):
    moments = lax.psum(jnp.stack([jnp.sum(x_f, axis=-1), jnp.sum(x_f * x_f, axis=-1)]), "tx")
    mean = (moments[0] / width)[..., None]
    variance = (moments[1] / width)[..., None] - mean * mean
    return ((x_f - mean) * lax.rsqrt(variance + EPS) * gain + shift).astype(jnp.bfloat16)


def solution(mesh):
    tx_size = mesh.shape["tx"]
    act_spec = P("dp", None, "tx")
    vec_tx = P(None, "tx")
    proj_spec = P(None, "tx", "ty", None)
    head_vec = P(None, "ty", None)
    in_specs = (act_spec, vec_tx, vec_tx, proj_spec, head_vec, proj_spec, proj_spec, head_vec,
                P(None, "ty", None, "tx"), vec_tx, vec_tx, vec_tx,
                P(None, "tx", "ty"), P(None, "ty"), P(None, "ty", "tx"), vec_tx)

    def local_fn(x_in, ln1_gain, ln1_bias, w_q, b_q, w_k, w_v, b_v, w_o, b_o, ln2_gain, ln2_bias, w_up, b_up, w_down, b_down):
        width = x_in.shape[-1] * tx_size
        scale = w_q.shape[-1] ** -0.5
        residual = x_in
        for layer in range(w_q.shape[0]):
            x_f = residual.astype(jnp.float32)
            normed = split_norm(x_f, ln1_gain[layer], ln1_bias[layer], width)
            part_q = jnp.einsum("bnw,whd->bnhd", normed, w_q[layer], preferred_element_type=jnp.float32).astype(jnp.bfloat16)
            part_k = jnp.einsum("bnw,whd->bnhd", normed, w_k[layer], preferred_element_type=jnp.float32).astype(jnp.bfloat16)
            part_v = jnp.einsum("bnw,whd->bnhd", normed, w_v[layer], preferred_element_type=jnp.float32).astype(jnp.bfloat16)
            sum_q, k_proj, sum_v = lax.psum((part_q, part_k, part_v), "tx")
            q_proj = (sum_q.astype(jnp.float32) + b_q[layer]).astype(jnp.bfloat16)
            v_proj = (sum_v.astype(jnp.float32) + b_v[layer]).astype(jnp.bfloat16)
            scores = jnp.einsum("bqhd,bkhd->bhqk", q_proj, k_proj, preferred_element_type=jnp.float32) * scale
            attn_prob = jax.nn.softmax(scores, axis=-1).astype(jnp.bfloat16)
            attended = jnp.einsum("bhqk,bkhd->bqhd", attn_prob, v_proj, preferred_element_type=jnp.float32).astype(jnp.bfloat16)
            part_o = jnp.einsum("bqhd,hdw->bqw", attended, w_o[layer], preferred_element_type=jnp.float32).astype(jnp.bfloat16)
            x_mid = (x_f + lax.psum(part_o, "ty").astype(jnp.float32) + b_o[layer]).astype(jnp.bfloat16)
            mid_f = x_mid.astype(jnp.float32)
            normed2 = split_norm(mid_f, ln2_gain[layer], ln2_bias[layer], width)
            part_up = jnp.einsum("bnw,wf->bnf", normed2, w_up[layer], preferred_element_type=jnp.float32).astype(jnp.bfloat16)
            hidden = jax.nn.gelu(lax.psum(part_up, "tx").astype(jnp.float32) + b_up[layer], approximate=True).astype(jnp.bfloat16)
            part_down = jnp.einsum("bnf,fw->bnw", hidden, w_down[layer], preferred_element_type=jnp.float32).astype(jnp.bfloat16)
            residual = (mid_f + lax.psum(part_down, "ty").astype(jnp.float32) + b_down[layer]).astype(jnp.bfloat16)
        return residual

    return jax.shard_map(local_fn, mesh=mesh, in_specs=in_specs, out_specs=act_spec, check_vma=False)
```

profile of v0, /device:TPU:97, one launch (start us, length us, event | category | flops | bytes accessed | tf_op | source)
XLA Modules:
  0.0 1711.1 jit_solution(14479113792098270307)
XLA Ops:
  6.6 7.1 convert_reduce_fusion.3
  14.5 1.4 fusion.159
  17.2 35.5 %all-reduce.15.cloned.1.call-done = f32[2,24,576]{2,1,0:T(8,128)} async-done(((f32[2,24,576]{2,1,0:T(8,128)}), f32[2,24,576]{2,1,0:T(8,128)}) %all-reduce.15.cloned.1.call-update) | async-done | bytes 110608 | tf_op jit(solution)/shard_map/psum | solution.py:10
  54.5 8.4 convolution_convert_fusion.6
  62.9 8.1 convolution_convert_fusion.5
  71.0 8.2 convolution_convert_fusion.7
  81.0 210.0 %all-reduce.37.cloned.1.call-done = (bf16[24,576,2,64]{1,3,2,0:T(8,128)(2,1)}, bf16[24,576,2,64]{1,3,2,0:T(8,128)(2,1)}, bf16[24,576,2,64]{1,3,2,0:T(8,128)(2,1)}) async-done(((bf16[24,576,2,64]{1,3,2,0:T(8,128)(2,1)}, bf16[24,576,2,64]{1,3,2,0:T(8,128)(2,1)}, bf16[24,576,2,64]{1,3,2,0:T(8,128)(2,1)}), (bf16[24,576,2,64]{1,3,2,0:T(8,128)(2,1)}, bf16[24,576,2,64]{1,3,2,0:T(8,128)(2,1)}, ...) | async-done | bytes 10616848 | tf_op jit(solution)/shard_map/psum | solution.py:36
  291.0 31.8 %fusion.162 = (f32[24,2,576]{2,1,0:T(2,128)S(1)}, f32[24,2,576,576]{2,3,1,0:T(8,128)}) fusion(bf16[24,576,2,64]{1,3,2,0:T(8,128)(2,1)} %get-tuple-element.16, bf16[24,576,2,64]{1,3,2,0:T(8,128)(2,1)} %get-tuple-element.17, f32[2,64]{1,0:T(2,128)S(1)} %get-tuple-element.33), kind=kOutput, calls=%fused_computation.191 | convolution fusion | flops 2091516416 | bytes 70889984 | tf_op jit(solution)/shard_map/sub | solution.py:40
  322.8 27.9 %bitcast_convert_fusion.1 = bf16[24,576,256]{2,1,0:T(8,128)(2,1)} fusion(f32[24,2,576,576]{2,3,1,0:T(8,128)} %get-tuple-element.41, f32[24,2,576]{2,1,0:T(2,128)S(1)} %get-tuple-element.40, bf16[24,576,2,64]{1,3,2,0:T(8,128)(2,1)} %get-tuple-element.18, f32[2,64]{1,0:T(2,128)S(1)} %get-tuple-element.31, bf16[2,2,64,256]{3,2,1,0:T(8,128)(2,1)S(1)} %copy-done.25), kind=kOutput, calls=%fused_computation.79 | convolution fusion | flops 2986868736 | bytes 74507264 | tf_op jit(solution)/shard_map/bqhd,hdw->bqw/dot_general | solution.py:42
  351.9 85.2 %all-reduce.17.cloned.1.call-done = bf16[24,576,256]{2,1,0:T(8,128)(2,1)} async-done(((bf16[24,576,256]{2,1,0:T(8,128)(2,1)}), bf16[24,576,256]{2,1,0:T(8,128)(2,1)}) %all-reduce.17.cloned.1.call-update) | async-done | bytes 7077904 | tf_op jit(solution)/shard_map/psum | solution.py:43
  437.1 12.2 convert_reduce_fusion.2
  450.9 33.7 %all-reduce.19.cloned.1.call-done = f32[2,24,576]{2,1,0:T(8,128)} async-done(((f32[2,24,576]{2,1,0:T(8,128)}), f32[2,24,576]{2,1,0:T(8,128)}) %all-reduce.19.cloned.1.call-update) | async-done | bytes 110608 | tf_op jit(solution)/shard_map/psum | solution.py:10
  486.3 10.4 convolution_convert_fusion.1
  497.9 248.5 %all-reduce.21.cloned.1.call-done = bf16[24,576,512]{2,1,0:T(8,128)(2,1)} async-done(((bf16[24,576,512]{2,1,0:T(8,128)(2,1)}), bf16[24,576,512]{2,1,0:T(8,128)(2,1)}) %all-reduce.21.cloned.1.call-update) | async-done | bytes 14155792 | tf_op jit(solution)/shard_map/psum | solution.py:47
  746.5 16.3 fusion.76
  763.5 85.8 %all-reduce.23.cloned.1.call-done = bf16[24,576,256]{2,1,0:T(8,128)(2,1)} async-done(((bf16[24,576,256]{2,1,0:T(8,128)(2,1)}), bf16[24,576,256]{2,1,0:T(8,128)(2,1)}) %all-reduce.23.cloned.1.call-update) | async-done | bytes 7077904 | tf_op jit(solution)/shard_map/psum | solution.py:49
  849.3 12.2 convert_reduce_fusion.1
  862.5 34.2 %all-reduce.25.cloned.1.call-done = f32[2,24,576]{2,1,0:T(8,128)} async-done(((f32[2,24,576]{2,1,0:T(8,128)}), f32[2,24,576]{2,1,0:T(8,128)}) %all-reduce.25.cloned.1.call-update) | async-done | bytes 110608 | tf_op jit(solution)/shard_map/psum | solution.py:10
  898.4 8.3 convolution_convert_fusion.3
  906.8 8.2 convolution_convert_fusion.2
  915.0 8.2 convolution_convert_fusion.4
  923.3 211.6 %all-reduce.35.cloned.1.call-done = (bf16[24,576,2,64]{1,3,2,0:T(8,128)(2,1)}, bf16[24,576,2,64]{1,3,2,0:T(8,128)(2,1)}, bf16[24,576,2,64]{1,3,2,0:T(8,128)(2,1)}) async-done(((bf16[24,576,2,64]{1,3,2,0:T(8,128)(2,1)}, bf16[24,576,2,64]{1,3,2,0:T(8,128)(2,1)}, bf16[24,576,2,64]{1,3,2,0:T(8,128)(2,1)}), (bf16[24,576,2,64]{1,3,2,0:T(8,128)(2,1)}, bf16[24,576,2,64]{1,3,2,0:T(8,128)(2,1)}, ...) | async-done | bytes 10616848 | tf_op jit(solution)/shard_map/psum | solution.py:36
  1135.0 31.8 %fusion.163 = (f32[24,2,576]{2,1,0:T(2,128)S(1)}, f32[24,2,576,576]{2,3,1,0:T(8,128)}) fusion(bf16[24,576,2,64]{1,3,2,0:T(8,128)(2,1)} %get-tuple-element.13, bf16[24,576,2,64]{1,3,2,0:T(8,128)(2,1)} %get-tuple-element.14, f32[2,64]{1,0:T(2,128)S(1)} %copy-done.14), kind=kOutput, calls=%fused_computation.192 | convolution fusion | flops 2091516416 | bytes 70889984 | tf_op jit(solution)/shard_map/sub | solution.py:40
  1166.7 27.9 %bitcast_convert_fusion = bf16[24,576,256]{2,1,0:T(8,128)(2,1)} fusion(f32[24,2,576,576]{2,3,1,0:T(8,128)} %get-tuple-element.43, f32[24,2,576]{2,1,0:T(2,128)S(1)} %get-tuple-element.42, bf16[24,576,2,64]{1,3,2,0:T(8,128)(2,1)} %get-tuple-element.15, f32[2,64]{1,0:T(2,128)S(1)} %copy-done.11, bf16[2,2,64,256]{3,2,1,0:T(8,128)(2,1)S(1)} %copy-done.25), kind=kOutput, calls=%fused_computation.78 | convolution fusion | flops 2986868736 | bytes 74507264 | tf_op jit(solution)/shard_map/bqhd,hdw->bqw/dot_general | solution.py:42
  1195.0 86.1 %all-reduce.27.cloned.1.call-done = bf16[24,576,256]{2,1,0:T(8,128)(2,1)} async-done(((bf16[24,576,256]{2,1,0:T(8,128)(2,1)}), bf16[24,576,256]{2,1,0:T(8,128)(2,1)}) %all-reduce.27.cloned.1.call-update) | async-done | bytes 7077904 | tf_op jit(solution)/shard_map/psum | solution.py:43
  1281.1 12.2 convert_reduce_fusion
  1294.0 34.5 %all-reduce.29.cloned.1.call-done = f32[2,24,576]{2,1,0:T(8,128)} async-done(((f32[2,24,576]{2,1,0:T(8,128)}), f32[2,24,576]{2,1,0:T(8,128)}) %all-reduce.29.cloned.1.call-update) | async-done | bytes 110608 | tf_op jit(solution)/shard_map/psum | solution.py:10
  1330.2 10.4 convolution_convert_fusion
  1340.8 249.7 %all-reduce.31.cloned.1.call-done = bf16[24,576,512]{2,1,0:T(8,128)(2,1)} async-done(((bf16[24,576,512]{2,1,0:T(8,128)(2,1)}), bf16[24,576,512]{2,1,0:T(8,128)(2,1)}) %all-reduce.31.cloned.1.call-update) | async-done | bytes 14155792 | tf_op jit(solution)/shard_map/psum | solution.py:47
  1590.5 16.2 fusion.79
  1606.8 86.5 %all-reduce.33.cloned.1.call-done = bf16[24,576,256]{2,1,0:T(8,128)(2,1)} async-done(((bf16[24,576,256]{2,1,0:T(8,128)(2,1)}), bf16[24,576,256]{2,1,0:T(8,128)(2,1)}) %all-reduce.33.cloned.1.call-update) | async-done | bytes 7077904 | tf_op jit(solution)/shard_map/psum | solution.py:49
  1693.2 10.5 fusion.59
  (106 shorter events, 17.9 us)
Async XLA Ops:
  6.5 46.2 %all-reduce.15.cloned.1.call-start = ((), (), s32[]{:S(2)}) async-start(), calls=%async_computation | async-start | bytes 245760 | tf_op jit(solution)/shard_map/psum | solution.py:10
  13.7 49.1 %slice-start.2 = ((s8[7077888]{0:T(1024)(128)(4,1)}), s8[2883584]{0:T(1024)(128)(4,1)S(1)}, s32[]{:S(2)}) async-start(s8[7077888]{0:T(1024)(128)(4,1)} %bitcast.158), calls=%async_computation.14 | async-start | bytes 5767168
  13.7 49.1 %copy-start.21 = (bf16[2,256,2,64]{1,3,2,0:T(8,128)(2,1)S(1)}, bf16[2,256,2,64]{1,3,2,0:T(8,128)(2,1)}, u32[]{:S(2)}) copy-start(bf16[2,256,2,64]{1,3,2,0:T(8,128)(2,1)} %param.21) | copy-start | bytes 393220
  14.4 276.5 %all-reduce.37.cloned.1.call-start = ((), (), s32[]{:S(2)}) async-start(), calls=%async_computation.11 | async-start | bytes 23592960 | tf_op jit(solution)/shard_map/psum | solution.py:36
  79.3 357.8 %all-reduce.17.cloned.1.call-start = ((), (), s32[]{:S(2)}) async-start(), calls=%async_computation.1 | async-start | bytes 14155776 | tf_op jit(solution)/shard_map/psum | solution.py:43
  291.0 31.8 %copy-start.25 = (bf16[2,2,64,256]{3,2,1,0:T(8,128)(2,1)S(1)}, bf16[2,2,64,256]{3,2,1,0:T(8,128)(2,1)}, u32[]{:S(2)}) copy-start(bf16[2,2,64,256]{3,2,1,0:T(8,128)(2,1)} %param.24) | copy-start | bytes 393220
  350.6 99.6 %copy-start.7 = (f32[2,256]{1,0:T(2,128)S(1)}, f32[2,256]{1,0:T(2,128)}, u32[]{:S(2)}) copy-start(f32[2,256]{1,0:T(2,128)} %param.27) | copy-start | bytes 6148
  350.6 135.6 %copy-start.16 = (bf16[2,256,512]{2,1,0:T(8,128)(2,1)S(1)}, bf16[2,256,512]{2,1,0:T(8,128)(2,1)}, u32[]{:S(2)}) copy-start(bf16[2,256,512]{2,1,0:T(8,128)(2,1)} %param.28) | copy-start | bytes 1572868
  350.7 133.8 %all-reduce.19.cloned.1.call-start = ((), (), s32[]{:S(2)}) async-start(), calls=%async_computation.2 | async-start | bytes 245760 | tf_op jit(solution)/shard_map/psum | solution.py:10
  450.0 296.5 %all-reduce.21.cloned.1.call-start = ((), (), s32[]{:S(2)}) async-start(), calls=%async_computation.3 | async-start | bytes 28311552 | tf_op jit(solution)/shard_map/psum | solution.py:47
  496.7 249.8 %copy-start.18 = (bf16[2,512,256]{2,1,0:T(8,128)(2,1)S(1)}, bf16[2,512,256]{2,1,0:T(8,128)(2,1)}, u32[]{:S(2)}) copy-start(bf16[2,512,256]{2,1,0:T(8,128)(2,1)} %param.30) | copy-start | bytes 1572868
  496.7 352.6 %all-reduce.23.cloned.1.call-start = ((), (), s32[]{:S(2)}) async-start(), calls=%async_computation.4 | async-start | bytes 14155776 | tf_op jit(solution)/shard_map/psum | solution.py:49
  762.8 135.7 %copy-start.12 = (f32[1,256]{1,0:T(1,128)S(1)}, f32[1,256]{1,0:T(1,128)}, u32[]{:S(2)}) copy-start(f32[1,256]{1,0:T(1,128)} %get-tuple-element.34) | copy-start | bytes 3076
  762.8 135.7 %copy-start.13 = (f32[1,256]{1,0:T(1,128)S(1)}, f32[1,256]{1,0:T(1,128)}, u32[]{:S(2)}) copy-start(f32[1,256]{1,0:T(1,128)} %get-tuple-element.36) | copy-start | bytes 3076
  762.8 135.7 %copy-start.20 = (bf16[2,256,2,64]{1,3,2,0:T(8,128)(2,1)S(1)}, bf16[2,256,2,64]{1,3,2,0:T(8,128)(2,1)}, u32[]{:S(2)}) copy-start(bf16[2,256,2,64]{1,3,2,0:T(8,128)(2,1)} %param.19) | copy-start | bytes 393220
  762.8 133.9 %all-reduce.25.cloned.1.call-start = ((), (), s32[]{:S(2)}) async-start(), calls=%async_computation.5 | async-start | bytes 245760 | tf_op jit(solution)/shard_map/psum | solution.py:10
  861.5 45.3 %slice-start = ((s8[7077888]{0:T(1024)(128)(4,1)}), s8[2883584]{0:T(1024)(128)(4,1)S(1)}, s32[]{:S(2)}) async-start(s8[7077888]{0:T(1024)(128)(4,1)} %bitcast.156), calls=%async_computation.12 | async-start | bytes 5767168
  861.5 45.3 %copy-start.22 = (bf16[2,256,2,64]{1,3,2,0:T(8,128)(2,1)S(1)}, bf16[2,256,2,64]{1,3,2,0:T(8,128)(2,1)}, u32[]{:S(2)}) copy-start(bf16[2,256,2,64]{1,3,2,0:T(8,128)(2,1)} %param.21) | copy-start | bytes 393220
  862.2 272.8 %all-reduce.35.cloned.1.call-start = ((), (), s32[]{:S(2)}) async-start(), calls=%async_computation.10 | async-start | bytes 23592960 | tf_op jit(solution)/shard_map/psum | solution.py:36
  915.0 220.0 %copy-start.14 = (f32[2,64]{1,0:T(2,128)S(1)}, f32[2,64]{1,0:T(2,128)}, u32[]{:S(2)}) copy-start(f32[2,64]{1,0:T(2,128)} %get-tuple-element.32) | copy-start | bytes 1540
  923.3 357.8 %all-reduce.27.cloned.1.call-start = ((), (), s32[]{:S(2)}) async-start(), calls=%async_computation.6 | async-start | bytes 14155776 | tf_op jit(solution)/shard_map/psum | solution.py:43
  1135.0 31.8 %copy-start.11 = (f32[2,64]{1,0:T(2,128)S(1)}, f32[2,64]{1,0:T(2,128)}, u32[]{:S(2)}) copy-start(f32[2,64]{1,0:T(2,128)} %get-tuple-element.30) | copy-start | bytes 1540
  1166.7 114.4 %copy-start = (f32[1,256]{1,0:T(1,128)S(1)}, f32[1,256]{1,0:T(1,128)}, u32[]{:S(2)}) copy-start(f32[1,256]{1,0:T(1,128)} %get-tuple-element.39) | copy-start | bytes 3076
  1194.6 135.6 %copy-start.10 = (f32[1,256]{1,0:T(1,128)S(1)}, f32[1,256]{1,0:T(1,128)}, u32[]{:S(2)}) copy-start(f32[1,256]{1,0:T(1,128)} %get-tuple-element.26) | copy-start | bytes 3076
  1194.6 135.6 %copy-start.15 = (f32[1,256]{1,0:T(1,128)S(1)}, f32[1,256]{1,0:T(1,128)}, u32[]{:S(2)}) copy-start(f32[1,256]{1,0:T(1,128)} %get-tuple-element.28) | copy-start | bytes 3076
  1194.6 135.6 %copy-start.17 = (bf16[2,256,512]{2,1,0:T(8,128)(2,1)S(1)}, bf16[2,256,512]{2,1,0:T(8,128)(2,1)}, u32[]{:S(2)}) copy-start(bf16[2,256,512]{2,1,0:T(8,128)(2,1)} %param.28) | copy-start | bytes 1572868
  1194.7 133.8 %all-reduce.29.cloned.1.call-start = ((), (), s32[]{:S(2)}) async-start(), calls=%async_computation.7 | async-start | bytes 245760 | tf_op jit(solution)/shard_map/psum | solution.py:10
  1294.0 296.5 %all-reduce.31.cloned.1.call-start = ((), (), s32[]{:S(2)}) async-start(), calls=%async_computation.8 | async-start | bytes 28311552 | tf_op jit(solution)/shard_map/psum | solution.py:47
  1340.7 249.8 %copy-start.9 = (f32[1,512]{1,0:T(1,128)S(1)}, f32[1,512]{1,0:T(1,128)}, u32[]{:S(2)}) copy-start(f32[1,512]{1,0:T(1,128)} %get-tuple-element.22) | copy-start | bytes 6148
  1340.7 249.8 %copy-start.19 = (bf16[2,512,256]{2,1,0:T(8,128)(2,1)S(1)}, bf16[2,512,256]{2,1,0:T(8,128)(2,1)}, u32[]{:S(2)}) copy-start(bf16[2,512,256]{2,1,0:T(8,128)(2,1)} %param.30) | copy-start | bytes 1572868
  1340.7 352.5 %all-reduce.33.cloned.1.call-start = ((), (), s32[]{:S(2)}) async-start(), calls=%async_computation.9 | async-start | bytes 14155776 | tf_op jit(solution)/shard_map/psum | solution.py:49
  1590.5 102.7 %copy-start.1 = (f32[1,256]{1,0:T(1,128)S(1)}, f32[1,256]{1,0:T(1,128)}, u32[]{:S(2)}) copy-start(f32[1,256]{1,0:T(1,128)} %get-tuple-element.24) | copy-start | bytes 3076
  (10 other events, 125.0 us)
Sparse Core Ops, SparseCore 0:
  14.6 38.1 all-reduce.14
  79.4 211.5 all-reduce.36
  350.8 86.2 all-reduce.16
  450.1 34.3 all-reduce.18
  496.8 249.5 all-reduce.20
  763.0 86.2 all-reduce.22
  862.3 34.3 all-reduce.24
  923.4 211.5 all-reduce.34
  1194.8 86.2 all-reduce.26
  1294.1 34.3 all-reduce.28
  1340.8 249.5 all-reduce.30
  1606.9 86.2 all-reduce.32
where the time goes:
time: 1720 us; the launch traced here: 1710 us
  waiting for transfers between devices  1400 us (81%)
  matrix products  222 us (13%)
  other arithmetic  63.7 us (4%)
    psum x2, waiting for transfers between devices, local_fn(): lax.psum(part_up, 'tx').astype(jnp.float32) + b_up[layer]  498 us
    psum x2, waiting for transfers between devices, local_fn(): sum_q, k_proj, sum_v = lax.psum((part_q, part_k, part_v), 'tx')  422 us
    psum x2, waiting for transfers between devices, local_fn(): lax.psum(part_down, 'ty').astype(jnp.float32)  172 us
    psum x2, waiting for transfers between devices, local_fn(): lax.psum(part_o, 'ty').astype(jnp.float32)  171 us
    psum x4, waiting for transfers between devices, split_norm(): lax.psum(jnp.stack([jnp.sum(x_f, axis=-1), jnp.sum(x_f * x_f, axis=-1)]),...  138 us
    sub x2, matrix products, local_fn(): attn_prob = jax.nn.softmax(scores, axis=-1).astype(jnp.bfloat16)  63.5 us
    dot_general x2, matrix products, local_fn(): jnp.einsum('bqhd,hdw->bqw', attended, w_o[layer], preferred_element_type=...  55.7 us
    reduce_sum x4, other arithmetic, split_norm(): jnp.sum(x_f, axis=-1)  43.7 us
  transfers between devices with their start and end apart: 12, of which 12 were waited for; matrix products, arithmetic and copies ran while one was open for 0% of the time, Pallas kernels for 0%

commit v1 on v0

v1 whole, which is shorter than its diff:
```python
import functools
import math

import jax
import jax.numpy as jnp
from jax import lax
from jax.experimental import pallas as pl
from jax.experimental.pallas import tpu as pltpu
from jax.sharding import PartitionSpec as P

EPS = 1e-6
F32, BF16 = jnp.float32, jnp.bfloat16


def dot(a, b):
    return jnp.dot(a, b, preferred_element_type=F32)


def norm(x_f, gain, shift):
    mean = jnp.mean(x_f, axis=-1, keepdims=True)
    centred = x_f - mean
    variance = jnp.mean(centred * centred, axis=-1, keepdims=True)
    return (centred * lax.rsqrt(variance + EPS) * gain + shift).astype(BF16)


def norm_rows(x_ref, gain_ref, shift_ref, h_ref, rows):
    def body(r, _):
        at = pl.ds(pl.multiple_of(r * rows, rows), rows)
        h_ref[at, :] = norm(x_ref[at, :].astype(F32), gain_ref[...], shift_ref[...])
        return 0

    lax.fori_loop(0, x_ref.shape[0] // rows, body, 0)


def finish_rows(x_ref, acc_ref, bias_ref, out_ref, rows):
    def body(r, _):
        at = pl.ds(pl.multiple_of(r * rows, rows), rows)
        out_ref[at, :] = (x_ref[at, :].astype(F32) + acc_ref[at, :] + bias_ref[...]).astype(BF16)
        return 0

    lax.fori_loop(0, x_ref.shape[0] // rows, body, 0)


def attention_kernel(head, x_ref, gain_ref, shift_ref, wqkv_ref, bqkv_ref, wo_ref, bo_ref, out_ref, h_ref, qkv_ref, o_ref, acc_ref):
    step = pl.program_id(0)
    txs, _, depth, cols = wqkv_ref.shape
    tokens = x_ref.shape[0]
    pair = cols // 3

    @pl.when(step == 0)
    def _():
        norm_rows(x_ref, gain_ref, shift_ref, h_ref, 96)
        acc_ref[...] = jnp.zeros_like(acc_ref)

    for n in range(3):
        at = pl.ds(n * pair, pair)
        total = jnp.zeros((tokens, pair), F32)
        for t in range(txs):
            total += dot(h_ref[:, pl.ds(t * depth, depth)], wqkv_ref[t, 0, :, at])
        qkv_ref[:, at] = (total + bqkv_ref[0, :, at]).astype(BF16)

    scale = head ** -0.5 * math.log2(math.e)
    chunk = 192
    for c in range(tokens // chunk):
        rows = pl.ds(c * chunk, chunk)
        outs = []
        for hd in range(pair // head):
            q = qkv_ref[rows, pl.ds(hd * head, head)]
            k = qkv_ref[:, pl.ds(pair + hd * head, head)]
            v = qkv_ref[:, pl.ds(2 * pair + hd * head, head)]
            s = lax.dot_general(q, k, (((1,), (1,)), ((), ())), preferred_element_type=F32)
            e = jnp.exp2((s - jnp.max(s, axis=-1, keepdims=True)) * scale)
            p = (e * (1.0 / jnp.sum(e, axis=-1, keepdims=True))).astype(BF16)
            outs.append(dot(p, v))
        o_ref[rows, :] = jnp.concatenate(outs, axis=-1).astype(BF16)

    width = wo_ref.shape[3]
    for t in range(txs):
        at = pl.ds(t * width, width)
        acc_ref[:, at] += dot(o_ref[...], wo_ref[t, 0])

    @pl.when(step == pl.num_programs(0) - 1)
    def _():
        finish_rows(x_ref, acc_ref, bo_ref, out_ref, 96)


def mlp_kernel(x_ref, gain_ref, shift_ref, wup_ref, bup_ref, wdown_ref, bdown_ref, out_ref, h_ref, u_ref, acc_ref):
    step = pl.program_id(0)
    txs, _, depth, hidden = wup_ref.shape
    tokens = x_ref.shape[0]

    @pl.when(step == 0)
    def _():
        norm_rows(x_ref, gain_ref, shift_ref, h_ref, 96)
        acc_ref[...] = jnp.zeros_like(acc_ref)

    tile = 256
    for n in range(hidden // tile):
        at = pl.ds(n * tile, tile)
        total = jnp.zeros((tokens, tile), F32)
        for t in range(txs):
            total += dot(h_ref[:, pl.ds(t * depth, depth)], wup_ref[t, 0, :, at])
        u_ref[:, at] = jax.nn.gelu(total + bup_ref[0, :, at], approximate=True).astype(BF16)

    width = wdown_ref.shape[3]
    for t in range(txs):
        at = pl.ds(t * width, width)
        acc_ref[:, at] += dot(u_ref[...], wdown_ref[t, 0])

    @pl.when(step == pl.num_programs(0) - 1)
    def _():
        finish_rows(x_ref, acc_ref, bdown_ref, out_ref, 96)


def whole(a):
    return pl.BlockSpec(a.shape, lambda i: (0,) * a.ndim)


def per_step(a):
    return pl.BlockSpec((1,) + a.shape[1:], lambda i: (i,) + (0,) * (a.ndim - 1))


def blocks(a):
    return pl.BlockSpec((a.shape[0], 1) + a.shape[2:], lambda i: (0, i, 0, 0))


def attention_block(head, x, gain, shift, wqkv, bqkv, wo, bo):
    tokens, width = x.shape
    steps, cols = wqkv.shape[1], wqkv.shape[3]
    return pl.pallas_call(
        functools.partial(attention_kernel, head),
        out_shape=jax.ShapeDtypeStruct(x.shape, BF16),
        grid=(steps,),
        in_specs=[whole(x), whole(gain), whole(shift), blocks(wqkv), per_step(bqkv), blocks(wo), whole(bo)],
        out_specs=whole(x),
        scratch_shapes=[pltpu.VMEM((tokens, width), BF16), pltpu.VMEM((tokens, cols), BF16),
                        pltpu.VMEM((tokens, cols // 3), BF16), pltpu.VMEM((tokens, width), F32)],
        compiler_params=pltpu.CompilerParams(dimension_semantics=("arbitrary",), vmem_limit_bytes=48 << 20),
        cost_estimate=pl.CostEstimate(flops=20_000_000_000, bytes_accessed=10_000_000, transcendentals=5_000_000),
        name="attention_block",
    )(x, gain, shift, wqkv, bqkv, wo, bo)


def mlp_block(x, gain, shift, wup, bup, wdown, bdown):
    tokens, width = x.shape
    steps, hidden = wup.shape[1], wup.shape[3]
    return pl.pallas_call(
        mlp_kernel,
        out_shape=jax.ShapeDtypeStruct(x.shape, BF16),
        grid=(steps,),
        in_specs=[whole(x), whole(gain), whole(shift), blocks(wup), per_step(bup), blocks(wdown), whole(bdown)],
        out_specs=whole(x),
        scratch_shapes=[pltpu.VMEM((tokens, width), BF16), pltpu.VMEM((tokens, hidden), BF16), pltpu.VMEM((tokens, width), F32)],
        compiler_params=pltpu.CompilerParams(dimension_semantics=("arbitrary",), vmem_limit_bytes=48 << 20),
        cost_estimate=pl.CostEstimate(flops=20_000_000_000, bytes_accessed=18_000_000, transcendentals=2_000_000),
        name="mlp_block",
    )(x, gain, shift, wup, bup, wdown, bdown)


def solution(mesh):
    txs, tys = mesh.shape["tx"], mesh.shape["ty"]
    act_spec = P("dp", None, "tx")
    vec_tx = P(None, "tx")
    proj_spec = P(None, "tx", "ty", None)
    head_vec = P(None, "ty", None)
    in_specs = (act_spec, vec_tx, vec_tx, proj_spec, head_vec, proj_spec, proj_spec, head_vec,
                P(None, "ty", None, "tx"), vec_tx, vec_tx, vec_tx,
                P(None, "tx", "ty"), P(None, "ty"), P(None, "ty", "tx"), vec_tx)

    def local_fn(x_in, ln1_gain, ln1_bias, w_q, b_q, w_k, w_v, b_v, w_o, b_o, ln2_gain, ln2_bias, w_up, b_up, w_down, b_down):
        layers, depth, heads, head = w_q.shape
        imgs, tokens, part = x_in.shape
        width = part * txs
        each = imgs // tys
        pad = txs - each
        ty = lax.axis_index("ty")

        def gather(w):
            full = lax.all_gather(w, ("tx", "ty"), axis=0, tiled=False)
            return full.reshape((txs, tys) + w.shape)

        vecs = lax.all_gather(jnp.stack([ln1_gain, ln1_bias, b_o, ln2_gain, ln2_bias, b_down]), "tx", axis=2, tiled=True)
        pair = heads * head
        zero = jnp.zeros((layers, pair), F32)
        bias = lax.all_gather(jnp.concatenate([b_q.reshape(layers, pair), zero, b_v.reshape(layers, pair), b_up], axis=1), "ty", axis=1, tiled=False)
        bias = bias[:, :, None, :]

        mine = lax.dynamic_slice_in_dim(x_in, ty * each, each, 0)
        mine = jnp.concatenate([mine, mine[:pad]], axis=0)
        x = lax.all_to_all(mine, "tx", 0, 2, tiled=True).reshape(tokens, width)

        weights = []
        for layer in range(layers):
            qkv = jnp.concatenate([w[layer].reshape(depth, pair) for w in (w_q, w_k, w_v)], axis=1)
            weights.append((gather(qkv), gather(w_o[layer].reshape(pair, part)), gather(w_up[layer]), gather(w_down[layer])))
        for layer in range(layers):
            gain1, shift1, bo, gain2, shift2, bdown = (vecs[i, layer][None] for i in range(6))
            wqkv, wo, wup, wdown = weights[layer]
            x = attention_block(head, x, gain1, shift1, wqkv, bias[layer, ..., :3 * pair], wo, bo)
            x = mlp_block(x, gain2, shift2, wup, bias[layer, ..., 3 * pair:], wdown, bdown)
        y = lax.all_to_all(x.reshape(1, tokens, width), "tx", 2, 0, tiled=True)[:each]
        return lax.all_gather(y, "ty", axis=0, tiled=True)

    return jax.shard_map(local_fn, mesh=mesh, in_specs=in_specs, out_specs=act_spec, check_vma=False)
```

time: 1720 us -> 495 us (0.29)
  waiting for transfers between devices: 1400 us -> 268 us
  matrix products: 222 us -> 0 us
  Pallas kernels: 0 us -> 108 us
  other arithmetic: 63.7 us -> 12.4 us
  blocking collectives: 0 us -> 49.4 us
  local copies, waits for them, and re-layouts: 7.42 us -> 35 us
    psum x12 -> x0, waiting for transfers between devices: 1400 us -> none  [the longest x2 498 us: local_fn(): lax.psum(part_up, 'tx').astype(jnp.float32) + b_up[layer]]
    all_gather x0 -> x9, waiting for transfers between devices: none -> 266 us  [the longest x8 225 us: gather(): full = lax.all_gather(w, ('tx', 'ty'), axis=0, tiled=False)]
    dot_general x12 -> x0, matrix products: 158 us -> none  [the longest x2 55.7 us: local_fn(): jnp.einsum('bqhd,hdw->bqw', attended, w_o[layer], preferred_element_type=...]
    pallas_call x0 -> x4, Pallas kernels: none -> 108 us  [the longest x2 75.4 us: attention_block(): pl.pallas_call(functools.partial(attention_kernel, head), out_shape=jax.S...]
    sub x2 -> x0, matrix products: 63.5 us -> none  [local_fn(): attn_prob = jax.nn.softmax(scores, axis=-1).astype(jnp.bfloat16)]
    reduce_sum x4 -> x0, other arithmetic: 43.7 us -> none  [split_norm(): jnp.sum(x_f, axis=-1)]
    all_gather x0 -> x2, blocking collectives: none -> 29.7 us  [the longest x1 20.3 us: local_fn(): lax.all_gather(jnp.concatenate([b_q.reshape(layers, pair), zero, b_v.resh...]
    all_to_all x0 -> x1, blocking collectives: none -> 19.8 us  [local_fn(): lax.all_to_all(x.reshape(1, tokens, width), 'tx', 2, 0, tiled=True)[:each]]
  transfers between devices with their start and end apart: 12 -> 10, of which waited for: 12 -> 8; matrix products, arithmetic and copies ran while one was open for 0% -> 2% of each run, Pallas kernels for 0% -> 19%
where the time goes in v1:
time: 495 us; the launch traced here: 494 us
  waiting for transfers between devices  268 us (54%)
  Pallas kernels  108 us (22%)
  blocking collectives  49.4 us (10%)
  local copies, waits for them, and re-layouts  35 us (7%)
  between operations  13.6 us (3%)
  other arithmetic  12.4 us (3%)
  starting transfers between devices  7.07 us (1%)
    all_gather x8, waiting for transfers between devices, gather(): full = lax.all_gather(w, ('tx', 'ty'), axis=0, tiled=False)  225 us
    pallas_call x2, Pallas kernels, attention_block(): pl.pallas_call(functools.partial(attention_kernel, head), out_shape=jax.S...  75.4 us
    all_gather x1, waiting for transfers between devices, local_fn(): return lax.all_gather(y, 'ty', axis=0, tiled=True)  41.4 us
    pallas_call x2, Pallas kernels, mlp_block(): pl.pallas_call(mlp_kernel, out_shape=jax.ShapeDtypeStruct(x.shape, BF16),...  33 us
    all_gather x1, blocking collectives, local_fn(): lax.all_gather(jnp.concatenate([b_q.reshape(layers, pair), zero, b_v.resh...  20.3 us
    all_to_all x1, blocking collectives, local_fn(): lax.all_to_all(x.reshape(1, tokens, width), 'tx', 2, 0, tiled=True)[:each]  19.8 us
    unnamed x37, local copies, waits for them, and re-layouts  17.1 us
  transfers between devices with their start and end apart: 10, of which 8 were waited for; matrix products, arithmetic and copies ran while one was open for 2% of the time, Pallas kernels for 19%

profile of v1, /device:TPU:97, one launch (start us, length us, event | category | flops | bytes accessed | tf_op | source)
XLA Modules:
  0.0 494.3 jit_solution(16311678153971538249)
XLA Ops:
  6.6 1.6 fusion.2
  9.3 0.9 fusion.4
  17.5 1.0 constant_dynamic-slice_fusion
  18.5 1.2 constant_dynamic-slice_fusion.1
  19.8 1.1 pad_maximum_fusion
  21.0 6.6 %all-to-all-start = ((bf16[4,576,256]{2,1,0:T(8,128)(2,1)}), bf16[4,576,256]{2,1,0:T(8,128)(2,1)S(1)}, u32[]{:S(2)}, u32[]{:S(2)}) async-start(bf16[4,576,256]{2,1,0:T(8,128)(2,1)} %pad_maximum_fusion), calls=%async_computation | async-start | bytes 2359296 | tf_op jit(solution)/shard_map/all_to_all | solution.py:190
  27.8 20.3 %all-gather.1 = f32[2,7168]{1,0:T(2,128)S(1)} all-gather(f32[2,896]{1,0:T(2,128)S(1)} %pad_maximum_fusion.3), channel_id=3, replica_groups=mesh['dp'=1,'tx'=4,'ty'=8] {'ty'}, dimensions={1}, use_global_device_ids=true | all-gather | bytes 64512 | tf_op jit(solution)/shard_map/all_gather | solution.py:185
  48.3 9.4 %all_gather.42 = f32[6,2,1024]{2,1,0:T(2,128)S(1)} all-gather(f32[6,2,256]{2,1,0:T(2,128)S(1)} %constant_dynamic-update-slice_fusion), channel_id=1, replica_groups=mesh['dp'=1,'tx'=4,'ty'=8] {'tx'}, dimensions={2}, use_global_device_ids=true | all-gather | bytes 61440 | tf_op jit(solution)/shard_map/all_gather | solution.py:182
  57.8 0.9 copy.34
  59.0 40.8 %all-gather.26.cloned.1.call-done = bf16[8192,384]{1,0:T(8,128)(2,1)} async-done(((bf16[256,384]{1,0:T(8,128)(2,1)}), bf16[8192,384]{1,0:T(8,128)(2,1)}) %all-gather.26.cloned.1.call-update) | async-done | bytes 6291472 | tf_op jit(solution)/shard_map/all_gather | solution.py:179
  99.8 1.6 copy-done
  101.3 37.7 %attention_block.2.x_ref = bf16[576,1024]{1,0:T(8,128)(2,1)S(1)} custom-call(bf16[576,1024]{1,0:T(8,128)(2,1)S(1)} %bitcast.73, f32[1,1024]{1,0:T(1,128)S(1)} %get-tuple-element.32.gain_ref, f32[1,1024]{1,0:T(1,128)S(1)} %get-tuple-element.31.shift_ref, bf16[4,8,256,384]{3,2,1,0:T(8,128)(2,1)} %bitcast.96, f32[8,1,384]{2,1,0:T(1,128)S(1)} %get-tuple-element.20.bqkv_ref, ...), custom_call_target="tpu_custom_call" | custom-call | flops 20000000000 | bytes 10000000 | tf_op jit(solution)/shard_map/attention_block/pallas_call | solution.py:130
  139.1 8.9 %all-gather.16.cloned.1.call-done = bf16[32,256,512]{2,1,0:T(8,128)(2,1)} async-done(((bf16[1,256,512]{2,1,0:T(8,128)(2,1)}), bf16[32,256,512]{2,1,0:T(8,128)(2,1)}) %all-gather.16.cloned.1.call-update) | async-done | bytes 8388624 | tf_op jit(solution)/shard_map/all_gather | solution.py:179
  148.0 48.8 %all-gather.18.cloned.1.call-done = bf16[32,512,256]{2,1,0:T(8,128)(2,1)} async-done(((bf16[1,512,256]{2,1,0:T(8,128)(2,1)}), bf16[32,512,256]{2,1,0:T(8,128)(2,1)}) %all-gather.18.cloned.1.call-update) | async-done | bytes 8388624 | tf_op jit(solution)/shard_map/all_gather | solution.py:179
  196.8 16.5 %mlp_block.2.x_ref = bf16[576,1024]{1,0:T(8,128)(2,1)S(1)} custom-call(bf16[576,1024]{1,0:T(8,128)(2,1)S(1)} %attention_block.2.x_ref, f32[1,1024]{1,0:T(1,128)S(1)} %get-tuple-element.29.gain_ref, f32[1,1024]{1,0:T(1,128)S(1)} %get-tuple-element.28.shift_ref, bf16[4,8,256,512]{3,2,1,0:T(8,128)(2,1)} %bitcast.92, ...), custom_call_target="tpu_custom_call" | custom-call | flops 20000000000 | bytes 18000000 | tf_op jit(solution)/shard_map/mlp_block/pallas_call | solution.py:147
  213.4 23.3 %all-gather.20.cloned.1.call-done = bf16[32,128,256]{2,1,0:T(8,128)(2,1)} async-done(((bf16[1,128,256]{2,1,0:T(8,128)(2,1)}), bf16[32,128,256]{2,1,0:T(8,128)(2,1)}) %all-gather.20.cloned.1.call-update) | async-done | bytes 2097168 | tf_op jit(solution)/shard_map/all_gather | solution.py:179
  236.6 45.0 %all-gather.28.cloned.1.call-done = bf16[8192,384]{1,0:T(8,128)(2,1)} async-done(((bf16[256,384]{1,0:T(8,128)(2,1)}), bf16[8192,384]{1,0:T(8,128)(2,1)}) %all-gather.28.cloned.1.call-update) | async-done | bytes 6291472 | tf_op jit(solution)/shard_map/all_gather | solution.py:179
  281.6 1.6 copy-done.1
  283.2 37.7 %attention_block.3.x_ref = bf16[576,1024]{1,0:T(8,128)(2,1)S(1)} custom-call(bf16[576,1024]{1,0:T(8,128)(2,1)S(1)} %mlp_block.2.x_ref, f32[1,1024]{1,0:T(1,128)S(1)} %get-tuple-element.26.gain_ref, f32[1,1024]{1,0:T(1,128)S(1)} %get-tuple-element.25.shift_ref, bf16[4,8,256,384]{3,2,1,0:T(8,128)(2,1)} %bitcast.97, ...), custom_call_target="tpu_custom_call" | custom-call | flops 20000000000 | bytes 10000000 | tf_op jit(solution)/shard_map/attention_block/pallas_call | solution.py:130
  320.9 8.9 %all-gather.22.cloned.1.call-done = bf16[32,256,512]{2,1,0:T(8,128)(2,1)} async-done(((bf16[1,256,512]{2,1,0:T(8,128)(2,1)}), bf16[32,256,512]{2,1,0:T(8,128)(2,1)}) %all-gather.22.cloned.1.call-update) | async-done | bytes 8388624 | tf_op jit(solution)/shard_map/all_gather | solution.py:179
  329.8 49.0 %all-gather.24.cloned.1.call-done = bf16[32,512,256]{2,1,0:T(8,128)(2,1)} async-done(((bf16[1,512,256]{2,1,0:T(8,128)(2,1)}), bf16[32,512,256]{2,1,0:T(8,128)(2,1)}) %all-gather.24.cloned.1.call-update) | async-done | bytes 8388624 | tf_op jit(solution)/shard_map/all_gather | solution.py:179
  378.8 16.5 %mlp_block.3 = bf16[576,1024]{1,0:T(8,128)(2,1)S(1)} custom-call(bf16[576,1024]{1,0:T(8,128)(2,1)S(1)} %attention_block.3.x_ref, f32[1,1024]{1,0:T(1,128)S(1)} %get-tuple-element.23.gain_ref, f32[1,1024]{1,0:T(1,128)S(1)} %get-tuple-element.22.shift_ref, bf16[4,8,256,512]{3,2,1,0:T(8,128)(2,1)} %bitcast.94, f32[8,1,512]{2,1,0:T(1,128)S(1)} %get-tuple-element.17.bup_ref, ...), custom_call_target="tpu_custom_call" | custom-call | flops 20000000000 | bytes 18000000 | tf_op jit(solution)/shard_map/mlp_block/pallas_call | solution.py:147
  395.3 4.1 copy.41
  399.9 9.8 %reduce = bf16[1024,576]{1,0:T(8,128)(2,1)S(1)} reduce(bf16[1024,1,576]{2,1,0:T(2,128)(2,1)} %bitcast.77, bf16[]{:T(256)} %broadcast.2), dimensions={1}, to_apply=%bitcast.70.reduce_sub_computation | reduce | bytes 2359298
  409.7 1.6 reshape.58
  411.3 19.8 %all_to_all.30 = bf16[4,2,73728]{2,1,0:T(2,128)(2,1)} all-to-all(bf16[4,2,73728]{2,1,0:T(2,128)(2,1)S(1)} %reshape.58), channel_id=1, replica_groups=mesh['dp'=1,'tx'=4,'ty'=8] {'tx'}, dimensions={0} | all-to-all | bytes 2359296 | tf_op jit(solution)/shard_map/all_to_all | solution.py:201
  431.1 3.5 reshape.59
  434.6 1.3 copy.45
  435.9 2.7 copy.44
  438.6 1.0 copy.43
  439.7 41.4 %all-gather.30.cloned.1.call-done = bf16[24,1,576,256]{3,2,1,0:T(8,128)(2,1)} async-done(((bf16[3,1,576,256]{3,2,1,0:T(8,128)(2,1)}), bf16[24,1,576,256]{3,2,1,0:T(8,128)(2,1)}) %all-gather.30.cloned.1.call-update) | async-done | bytes 7077904 | tf_op jit(solution)/shard_map/all_gather | solution.py:202
  481.1 6.7 %copy.53 = bf16[24,576,256]{2,1,0:T(8,128)(2,1)} copy(bf16[24,576,256]{2,1,0:T(8,128)(2,1)} %bitcast.79) | data formatting | bytes 14155776
  (73 shorter events, 9.5 us)
Async XLA Ops:
  6.5 5.7 %copy-start.2 = (bf16[2,256,512]{2,1,0:T(8,128)(2,1)S(1)}, bf16[2,256,512]{2,1,0:T(8,128)(2,1)}, u32[]{:S(2)}) copy-start(bf16[2,256,512]{2,1,0:T(8,128)(2,1)} %param.28) | copy-start | bytes 1572868
  6.5 52.4 %all-gather.14.cloned.1.call-start = ((), (), s32[]{:S(2)}) async-start(), calls=%async_computation.2 | async-start | bytes 2162688 | tf_op jit(solution)/shard_map/all_gather | solution.py:179
  8.2 91.6 %all-gather.26.cloned.1.call-start = ((), (), s32[]{:S(2)}) async-start(), calls=%async_computation.8 | async-start | bytes 6488064 | tf_op jit(solution)/shard_map/all_gather | solution.py:179
  9.3 3.9 copy-start.3
  12.1 135.9 %all-gather.16.cloned.1.call-start = ((), (), s32[]{:S(2)}) async-start(), calls=%async_computation.3 | async-start | bytes 8650752 | tf_op jit(solution)/shard_map/all_gather | solution.py:179
  13.1 183.7 %all-gather.18.cloned.1.call-start = ((), (), s32[]{:S(2)}) async-start(), calls=%async_computation.4 | async-start | bytes 8650752 | tf_op jit(solution)/shard_map/all_gather | solution.py:179
  14.1 222.5 %all-gather.20.cloned.1.call-start = ((), (), s32[]{:S(2)}) async-start(), calls=%async_computation.5 | async-start | bytes 2162688 | tf_op jit(solution)/shard_map/all_gather | solution.py:179
  14.7 266.8 %all-gather.28.cloned.1.call-start = ((), (), s32[]{:S(2)}) async-start(), calls=%async_computation.9 | async-start | bytes 6488064 | tf_op jit(solution)/shard_map/all_gather | solution.py:179
  15.9 313.9 %all-gather.22.cloned.1.call-start = ((), (), s32[]{:S(2)}) async-start(), calls=%async_computation.6 | async-start | bytes 8650752 | tf_op jit(solution)/shard_map/all_gather | solution.py:179
  16.7 362.0 %all-gather.24.cloned.1.call-start = ((), (), s32[]{:S(2)}) async-start(), calls=%async_computation.7 | async-start | bytes 8650752 | tf_op jit(solution)/shard_map/all_gather | solution.py:179
  20.9 6.7 %copy-start.5 = (f32[2,2,64]{2,1,0:T(2,128)S(1)}, f32[2,2,64]{2,1,0:T(2,128)}, u32[]{:S(2)}) copy-start(f32[2,2,64]{2,1,0:T(2,128)} %param.20) | copy-start | bytes 3076
  20.9 6.8 %copy-start.6 = (f32[2,2,64]{2,1,0:T(2,128)S(1)}, f32[2,2,64]{2,1,0:T(2,128)}, u32[]{:S(2)}) copy-start(f32[2,2,64]{2,1,0:T(2,128)} %param.23) | copy-start | bytes 3076
  20.9 6.9 %copy-start.4 = (f32[2,512]{1,0:T(2,128)S(1)}, f32[2,512]{1,0:T(2,128)}, u32[]{:S(2)}) copy-start(f32[2,512]{1,0:T(2,128)} %param.29) | copy-start | bytes 12292
  20.9 27.3 %copy-start.7 = (f32[2,256]{1,0:T(2,128)S(1)}, f32[2,256]{1,0:T(2,128)}, u32[]{:S(2)}) copy-start(f32[2,256]{1,0:T(2,128)} %param.17) | copy-start | bytes 6148
  20.9 27.3 %copy-start.8 = (f32[2,256]{1,0:T(2,128)S(1)}, f32[2,256]{1,0:T(2,128)}, u32[]{:S(2)}) copy-start(f32[2,256]{1,0:T(2,128)} %param.18) | copy-start | bytes 6148
  20.9 27.3 %copy-start.9 = (f32[2,256]{1,0:T(2,128)S(1)}, f32[2,256]{1,0:T(2,128)}, u32[]{:S(2)}) copy-start(f32[2,256]{1,0:T(2,128)} %param.25) | copy-start | bytes 6148
  20.9 27.3 %copy-start.10 = (f32[2,256]{1,0:T(2,128)S(1)}, f32[2,256]{1,0:T(2,128)}, u32[]{:S(2)}) copy-start(f32[2,256]{1,0:T(2,128)} %param.26) | copy-start | bytes 6148
  20.9 27.3 %copy-start.11 = (f32[2,256]{1,0:T(2,128)S(1)}, f32[2,256]{1,0:T(2,128)}, u32[]{:S(2)}) copy-start(f32[2,256]{1,0:T(2,128)} %param.27) | copy-start | bytes 6148
  20.9 27.3 %copy-start.12 = (f32[2,256]{1,0:T(2,128)S(1)}, f32[2,256]{1,0:T(2,128)}, u32[]{:S(2)}) copy-start(f32[2,256]{1,0:T(2,128)} %param.31) | copy-start | bytes 6148
  21.0 36.8 %all-to-all-start = ((bf16[4,576,256]{2,1,0:T(8,128)(2,1)}), bf16[4,576,256]{2,1,0:T(8,128)(2,1)S(1)}, u32[]{:S(2)}, u32[]{:S(2)}) async-start(bf16[4,576,256]{2,1,0:T(8,128)(2,1)} %pad_maximum_fusion), calls=%async_computation | async-start | bytes 2359296 | tf_op jit(solution)/shard_map/all_to_all | solution.py:190
  27.6 453.5 %all-gather.30.cloned.1.call-start = ((), (), s32[]{:S(2)}) async-start(), calls=%async_computation.10 | async-start | bytes 7962624 | tf_op jit(solution)/shard_map/all_gather | solution.py:202
  99.8 1.6 copy-start
  281.6 1.6 copy-start.1
Sparse Core Ops, SparseCore 0:
  9.4 44.9 all-gather.13
  56.5 43.2 all-gather.25
  101.8 46.1 all-gather.15
  149.9 46.8 all-gather.17
  198.7 37.8 all-gather.19
  238.5 42.9 all-gather.27
  283.7 46.0 all-gather.21
  331.9 46.8 all-gather.23
  439.8 41.2 all-gather.29

commit v2 on v0

v2 whole, which is shorter than its diff:
```python
import functools
import math

import jax
import jax.numpy as jnp
from jax import lax
from jax.experimental import pallas as pl
from jax.experimental.pallas import tpu as pltpu
from jax.sharding import PartitionSpec as P

EPS = 1e-6
F32, BF16 = jnp.float32, jnp.bfloat16
MESH = pl.DeviceIdType.MESH
CORES = 2
STEPS = {"xp": (1, 0), "xm": (-1, 0), "yp": (0, 1), "ym": (0, -1)}
ALL, A, B = (0, 2), (0, 1), (1, 1)
PLUS, MINUS = (0, 1), (1, 1)
PHASES = (
    [("xp", (0, 0), ALL, ALL), ("yp", (0, 0), ALL, ALL), ("xm", (0, 0), ALL, ALL), ("ym", (0, 0), ALL, ALL),
     ("sib", (0, 0), ALL, ALL)],
    [("xp", (-1, 0), ALL, PLUS), ("yp", (0, -1), ALL, PLUS), ("xm", (1, 0), ALL, MINUS), ("ym", (0, 1), ALL, MINUS),
     ("xp", (0, -1), B, ALL), ("yp", (-1, 0), A, ALL), ("xm", (0, -1), B, ALL), ("ym", (-1, 0), A, ALL),
     ("xp", (0, 1), B, ALL), ("yp", (1, 0), A, ALL), ("xm", (0, 1), B, ALL), ("ym", (1, 0), A, ALL),
     ("sib", (-1, 0), ALL, ALL), ("sib", (1, 0), ALL, ALL), ("sib", (0, -1), ALL, ALL), ("sib", (0, 1), ALL, ALL)],
    [("xp", (0, 2), B, ALL), ("yp", (2, 0), A, ALL), ("xm", (0, 2), B, ALL), ("ym", (2, 0), A, ALL),
     ("xp", (-1, -1), B, PLUS), ("yp", (-1, -1), A, PLUS), ("xm", (1, -1), B, MINUS), ("ym", (-1, 1), A, MINUS),
     ("xp", (-1, 1), B, PLUS), ("yp", (1, -1), A, PLUS), ("xm", (1, 1), B, MINUS), ("ym", (1, 1), A, MINUS),
     ("sib", (2, 0), ALL, ALL), ("sib", (0, 2), ALL, ALL), ("sib", (-1, -1), ALL, ALL), ("sib", (1, -1), ALL, ALL),
     ("sib", (-1, 1), ALL, ALL), ("sib", (1, 1), ALL, ALL)],
    [("xp", (-1, 2), B, PLUS), ("yp", (2, -1), A, PLUS), ("xm", (1, 2), B, MINUS), ("ym", (2, 1), A, MINUS),
     ("sib", (-1, 2), ALL, ALL), ("sib", (1, 2), ALL, ALL), ("sib", (2, -1), ALL, ALL), ("sib", (2, 1), ALL, ALL)],
    [("sib", (2, 2), ALL, ALL)],
)
SENT = ((5, 1), (5, 2), (5, 2), (5, 1), (1, 1))
FIRST = [sum(len(p) for p in PHASES[:i]) for i in range(len(PHASES) + 1)]
BEFORE = [(0, 0), (1, 0), (0, 1), (2, 0), (1, 1), (3, 0), (0, 2), (4, 0), (5, 0)]
SLOTS = (
    {0: [(2, 1)], 1: [(1, 2)], 2: [(3, 1), (0, 3)], 3: [(4, 1), (2, 2)], 4: [(1, 3)], 5: [(3, 2), (0, 4)], 6: [(4, 2)], 7: [(2, 3)]},
    {0: [(5, 1), (5, 2)], 1: [(1, 4)], 3: [(3, 3), (0, 5)], 5: [(4, 3)], 7: [(2, 4)]},
    {0: [(5, 3), (1, 5)], 1: [(3, 4)], 2: [(4, 4), (2, 5)], 4: [(3, 5)], 5: [(4, 5)]},
    {0: [(5, 4), (5, 5)]},
)


def dot(a, b):
    return jnp.dot(a, b, preferred_element_type=F32)


def kernel(head, each, w_ref, vec_ref, bias_ref, x_hbm, out_ref, g_ref,
           x_ref, h_ref, acc_ref, qkv_ref, o_ref, u_ref, wbuf, vecs, biases,
           send_sem, recv_sem, own_sem, load_sem, vec_send, vec_recv, bias_send, bias_recv,
           xin_send, xin_recv, o1_send, o1_recv, ring_send, ring_recv):
    groups, tys, txs = g_ref.shape[:3]
    nx, ny = tys // CORES, txs
    tokens, part = x_ref.shape[1:]
    me_t, me_s = lax.axis_index("tx"), lax.axis_index("ty")
    my_x, my_c = me_s // CORES, lax.rem(me_s, CORES)
    sibling = my_x * CORES + (CORES - 1 - my_c)
    worker = me_t < each

    def ty_at(dx):
        return lax.rem(my_x + dx + nx, nx) * CORES + my_c

    def tx_at(dy):
        return lax.rem(me_t + dy + ny, ny)

    def target(to):
        if to == "sib":
            return {"ty": sibling}
        dx, dy = STEPS[to]
        return {"ty": ty_at(dx)} if dx else {"tx": tx_at(dy)}

    barrier = pltpu.get_barrier_semaphore()
    for k in range(1, txs):
        pl.semaphore_signal(barrier, inc=1, device_id={"tx": tx_at(k)}, device_id_type=MESH)
    for k in range(1, tys):
        pl.semaphore_signal(barrier, inc=1, device_id={"ty": lax.rem(me_s + k, tys)}, device_id_type=MESH)
    pl.semaphore_wait(barrier, txs - 1 + tys - 1)

    def piece(g, ty, tx, half, sign):
        return g_ref.at[g, ty, tx, pl.ds(*half), pl.ds(*sign)]

    def copy(phase, i, g):
        to, (dx, dy), half, sign = PHASES[phase][i]
        place = piece(g, ty_at(dx), tx_at(dy), half, sign)
        return pltpu.make_async_remote_copy(
            src_ref=w_ref.at[g] if phase == 0 else place, dst_ref=place, send_sem=send_sem.at[g, phase],
            recv_sem=recv_sem.at[g, FIRST[phase] + i], device_id=target(to), device_id_type=MESH)

    def arrival(phase, i, g):
        to, (dx, dy), half, sign = PHASES[phase][i]
        if to == "sib":
            ty = lax.rem(my_x + dx + nx, nx) * CORES + (CORES - 1 - my_c)
            place = piece(g, ty, tx_at(dy), half, sign)
        else:
            sx, sy = STEPS[to]
            place = piece(g, ty_at(dx - sx), tx_at(dy - sy), half, sign)
        return pltpu.make_async_remote_copy(
            src_ref=place, dst_ref=place, send_sem=send_sem.at[g, phase],
            recv_sem=recv_sem.at[g, FIRST[phase] + i], device_id=target(to), device_id_type=MESH)

    def event(phase, g):
        if phase == 5:
            for p in range(5):
                for i, c in enumerate(PHASES[p]):
                    if c[0] == "sib":
                        arrival(p, i, g).wait_recv()
            return
        if phase:
            for i, c in enumerate(PHASES[phase - 1]):
                if c[0] != "sib":
                    arrival(phase - 1, i, g).wait_recv()
        for i in range(len(PHASES[phase])):
            copy(phase, i, g).start()

    for e in BEFORE[:1]:
        event(*e)
    own = pltpu.make_async_copy(w_ref, g_ref.at[:, me_s, me_t], own_sem)
    own.start()

    def x_copy(j):
        return pltpu.make_async_remote_copy(
            src_ref=x_hbm.at[me_s * each + j], dst_ref=x_ref.at[me_t], send_sem=xin_send.at[j],
            recv_sem=xin_recv.at[me_t], device_id={"tx": j}, device_id_type=MESH)

    def x_local():
        return pltpu.make_async_copy(x_hbm.at[me_s * each + me_t], x_ref.at[me_t], xin_recv.at[me_t])

    for j in range(each):
        @pl.when(me_t != j)
        def _():
            x_copy(j).start()

        @pl.when(me_t == j)
        def _():
            x_local().start()

    def vec_copy(k):
        return pltpu.make_async_remote_copy(
            src_ref=vec_ref, dst_ref=vecs.at[me_t], send_sem=vec_send.at[k], recv_sem=vec_recv.at[k],
            device_id={"tx": tx_at(k)}, device_id_type=MESH)

    def bias_copy(k):
        return pltpu.make_async_remote_copy(
            src_ref=bias_ref, dst_ref=biases.at[me_s], send_sem=bias_send.at[k], recv_sem=bias_recv.at[k],
            device_id={"ty": lax.rem(me_s + k, tys)}, device_id_type=MESH)

    for k in range(1, txs):
        vec_copy(k).start()
    for k in range(1, tys):
        bias_copy(k).start()
    vecs[me_t] = vec_ref[...]
    biases[me_s] = bias_ref[...]

    for e in BEFORE[1:]:
        event(*e)

    for k in range(1, txs):
        vec_copy(k).wait()
    for k in range(1, tys):
        bias_copy(k).wait()
    own.wait()

    @pl.when(worker)
    def _():
        for m in range(txs):
            pltpu.make_async_copy(x_hbm.at[0], x_ref.at[m], xin_recv.at[m]).wait()

    def vec(row):
        return jnp.concatenate([vecs[t, pl.ds(row, 1), :] for t in range(txs)], axis=-1)

    def norm(gain_row, shift_row):
        rows = 96

        def body(r, _):
            at = pl.ds(pl.multiple_of(r * rows, rows), rows)
            x_f = jnp.concatenate([x_ref[t, at, :] for t in range(txs)], axis=-1).astype(F32)
            mean = jnp.mean(x_f, axis=-1, keepdims=True)
            centred = x_f - mean
            variance = jnp.mean(centred * centred, axis=-1, keepdims=True)
            h = (centred * lax.rsqrt(variance + EPS) * vec(gain_row) + vec(shift_row)).astype(BF16)
            for t in range(txs):
                h_ref[t, at, :] = h[:, t * part:(t + 1) * part]
                acc_ref[t, at, :] = jnp.zeros((rows, part), F32)
            return 0

        lax.fori_loop(0, tokens // rows, body, 0)

    def finish(bias_row):
        rows = 96

        def body(r, _):
            at = pl.ds(pl.multiple_of(r * rows, rows), rows)
            for t in range(txs):
                x_ref[t, at, :] = (x_ref[t, at, :].astype(F32) + acc_ref[t, at, :] + vecs[t, pl.ds(bias_row, 1), :]).astype(BF16)
            return 0

        lax.fori_loop(0, tokens // rows, body, 0)

    depth = 4 * g_ref.shape[5]
    pair = o_ref.shape[1]

    def block(slot, which, t, columns):
        part_of = wbuf[slot, which, t, :, :, :, columns]
        return part_of.reshape(depth, part_of.shape[-1])

    def loads(slot, g, step, count):
        return [pltpu.make_async_copy(g_ref.at[g + i, step], wbuf.at[slot, i], load_sem.at[slot, i]) for i in range(count)]

    def run(slots, g, count, body):
        @pl.when(worker)
        def _():
            for c in ():
                c.start()

        def step_body(step, _):
            slot = lax.rem(step, 2)
            for s, events in slots.items():
                @pl.when(step == s)
                def _(events=events):
                    for e in events:
                        event(*e)

            @pl.when(worker)
            def _():
                @pl.when(step == 0)
                def _():
                    for c in loads(slot, g, step, count):
                        c.start()

                @pl.when(step + 1 < tys)
                def _():
                    for c in loads(1 - slot, g, step + 1, count):
                        c.start()
                for c in loads(slot, g, step, count):
                    c.wait()
                body(step, slot)
            return 0

        lax.fori_loop(0, tys, step_body, 0)

    def attention(layer, step, slot):
        for n in range(3):
            at = pl.ds(n * pair, pair)
            total = jnp.zeros((tokens, pair), F32)
            for t in range(txs):
                total += dot(h_ref[t], block(slot, 0, t, at))
            qkv_ref[:, at] = (total + biases[step, pl.ds(layer, 1), at]).astype(BF16)

        scale = head ** -0.5 * math.log2(math.e)
        chunk = 192
        for c in range(tokens // chunk):
            rows = pl.ds(c * chunk, chunk)
            outs = []
            for hd in range(pair // head):
                q = qkv_ref[rows, pl.ds(hd * head, head)]
                k = qkv_ref[:, pl.ds(pair + hd * head, head)]
                v = qkv_ref[:, pl.ds(2 * pair + hd * head, head)]
                s = lax.dot_general(q, k, (((1,), (1,)), ((), ())), preferred_element_type=F32)
                e = jnp.exp2((s - jnp.max(s, axis=-1, keepdims=True)) * scale)
                p = (e * (1.0 / jnp.sum(e, axis=-1, keepdims=True))).astype(BF16)
                outs.append(dot(p, v))
            o_ref[rows, :] = jnp.concatenate(outs, axis=-1).astype(BF16)

        for t in range(txs):
            w = block(slot, 0, t, pl.ds(3 * pair, part - pair))
            wo = jnp.concatenate([w[i * pair:(i + 1) * pair] for i in range(part // pair)], axis=1)
            acc_ref[t] += dot(o_ref[...], wo)

    def mlp(layer, step, slot):
        hidden = u_ref.shape[1]
        for n in range(hidden // part):
            at = pl.ds(n * part, part)
            total = jnp.zeros((tokens, part), F32)
            for t in range(txs):
                total += dot(h_ref[t], block(slot, 0, t, at))
            bias = biases[step, pl.ds(layer, 1), pl.ds(3 * pair + n * part, part)]
            u_ref[:, at] = jax.nn.gelu(total + bias, approximate=True).astype(BF16)
        for t in range(txs):
            total = acc_ref[t]
            for n in range(hidden // depth):
                total += dot(u_ref[:, pl.ds(n * depth, depth)], block(slot, 1, t, pl.ds(n * part, part)))
            acc_ref[t] = total

    layers = groups // 3
    for layer in range(layers):
        row = 6 * layer

        @pl.when(worker)
        def _():
            norm(row, row + 1)
        run(SLOTS[2 * layer], 3 * layer, 1, functools.partial(attention, layer))

        @pl.when(worker)
        def _():
            finish(row + 2)
            norm(row + 3, row + 4)
        run(SLOTS[2 * layer + 1], 3 * layer + 1, 2, functools.partial(mlp, layer))

        @pl.when(worker)
        def _():
            finish(row + 5)

    def o1_copy(k):
        return pltpu.make_async_remote_copy(
            src_ref=x_ref.at[tx_at(k)], dst_ref=out_ref.at[me_s * each + me_t], send_sem=o1_send.at[k],
            recv_sem=o1_recv.at[me_t], device_id={"tx": tx_at(k)}, device_id_type=MESH)

    def o1_local():
        return pltpu.make_async_copy(x_ref.at[me_t], out_ref.at[me_s * each + me_t], o1_recv.at[me_t])

    @pl.when(worker)
    def _():
        for k in range(1, txs):
            o1_copy(k).start()
        o1_local().start()

    half = tokens // 2
    every, first, second = pl.ds(0, tokens), pl.ds(0, half), pl.ds(half, half)
    ring = (("xp", 0, every), ("xm", 0, every), ("sib", 0, every),
            ("xp", -1, first), ("xm", 1, second), ("sib", -1, every), ("sib", 1, every), ("sib", 2, every))

    def ring_copy(kind, m):
        to, dx, rows = ring[kind]
        place = out_ref.at[ty_at(dx) * each + m, rows]
        return pltpu.make_async_remote_copy(
            src_ref=place, dst_ref=place, send_sem=ring_send.at[kind, m], recv_sem=ring_recv.at[kind, m],
            device_id=target(to), device_id_type=MESH)

    def ring_arrival(kind, m):
        to, dx, rows = ring[kind]
        if to == "sib":
            ty = lax.rem(my_x + dx + nx, nx) * CORES + (CORES - 1 - my_c)
        else:
            ty = ty_at(dx - STEPS[to][0])
        place = out_ref.at[ty * each + m, rows]
        return pltpu.make_async_remote_copy(
            src_ref=place, dst_ref=place, send_sem=ring_send.at[kind, m], recv_sem=ring_recv.at[kind, m],
            device_id=target(to), device_id_type=MESH)

    for m in range(each):
        place = out_ref.at[me_s * each + m]
        pltpu.make_async_copy(x_ref.at[0], place, o1_recv.at[m]).wait()
        for kind in (0, 1, 2):
            ring_copy(kind, m).start()
    for m in range(each):
        ring_arrival(0, m).wait_recv()
        ring_copy(3, m).start()
        ring_copy(5, m).start()
        ring_arrival(1, m).wait_recv()
        ring_copy(4, m).start()
        ring_copy(6, m).start()
    for m in range(each):
        ring_arrival(3, m).wait_recv()
        ring_arrival(4, m).wait_recv()
        ring_copy(7, m).start()
    for m in range(each):
        for kind in (2, 5, 6, 7):
            ring_arrival(kind, m).wait_recv()

    for m in range(each):
        for kind in range(len(ring)):
            ring_copy(kind, m).wait_send()
    for j in range(each):
        @pl.when(me_t != j)
        def _():
            x_copy(j).wait_send()

    @pl.when(worker)
    def _():
        for k in range(1, txs):
            o1_copy(k).wait_send()
    for g in range(groups):
        for phase, (a, b) in enumerate(SENT):
            place = g_ref.at[g, pl.ds(0, a), pl.ds(0, b)]
            pltpu.make_async_remote_copy(
                src_ref=place, dst_ref=place, send_sem=send_sem.at[g, phase], recv_sem=recv_sem.at[g, 0],
                device_id={"ty": sibling}, device_id_type=MESH).wait_send()


def solution(mesh):
    txs, tys = mesh.shape["tx"], mesh.shape["ty"]
    act_spec = P("dp", None, "tx")
    vec_tx = P(None, "tx")
    proj_spec = P(None, "tx", "ty", None)
    head_vec = P(None, "ty", None)
    in_specs = (act_spec, vec_tx, vec_tx, proj_spec, head_vec, proj_spec, proj_spec, head_vec,
                P(None, "ty", None, "tx"), vec_tx, vec_tx, vec_tx,
                P(None, "tx", "ty"), P(None, "ty"), P(None, "ty", "tx"), vec_tx)

    def local_fn(x_in, ln1_gain, ln1_bias, w_q, b_q, w_k, w_v, b_v, w_o, b_o, ln2_gain, ln2_bias, w_up, b_up, w_down, b_down):
        layers, depth, heads, head = w_q.shape
        imgs, tokens, part = x_in.shape
        hidden = w_up.shape[2]
        each, pair = imgs // tys, heads * head

        qkv = [w.reshape(layers, depth, pair) for w in (w_q, w_k, w_v)]
        wo = w_o.reshape(layers, pair, part)
        wo = jnp.concatenate([wo[:, :, i * pair:(i + 1) * pair] for i in range(part // pair)], axis=1)
        down = jnp.concatenate([w_down[:, i * depth:(i + 1) * depth] for i in range(hidden // depth)], axis=2)
        packed = jnp.stack([jnp.concatenate(qkv + [wo], axis=2), w_up, down], axis=1)
        groups = 3 * layers
        packed = packed.reshape(groups, 2, 2, depth // 4, hidden)

        vec = jnp.stack([ln1_gain, ln1_bias, b_o, ln2_gain, ln2_bias, b_down], axis=1).reshape(6 * layers, part)
        vec = jnp.pad(vec, ((0, -vec.shape[0] % 8), (0, 0)))
        bias = jnp.concatenate([b_q.reshape(layers, pair), jnp.zeros((layers, pair), F32), b_v.reshape(layers, pair), b_up], axis=1)
        bias = jnp.pad(bias, ((0, -layers % 8), (0, 0)))

        vmem = pl.BlockSpec(memory_space=pltpu.VMEM)
        hbm = pl.BlockSpec(memory_space=pl.ANY)
        dma = pltpu.SemaphoreType.DMA
        out, _ = pl.pallas_call(
            functools.partial(kernel, head, each),
            out_shape=(jax.ShapeDtypeStruct(x_in.shape, BF16),
                       jax.ShapeDtypeStruct((groups, tys, txs) + packed.shape[1:], BF16)),
            in_specs=[vmem, vmem, vmem, hbm],
            out_specs=(hbm, hbm),
            scratch_shapes=[
                pltpu.VMEM((txs, tokens, part), BF16), pltpu.VMEM((txs, tokens, part), BF16), pltpu.VMEM((txs, tokens, part), F32),
                pltpu.VMEM((tokens, 3 * pair), BF16), pltpu.VMEM((tokens, pair), BF16), pltpu.VMEM((tokens, hidden), BF16),
                pltpu.VMEM((2, 2, txs) + packed.shape[1:], BF16),
                pltpu.VMEM((txs,) + vec.shape, F32), pltpu.VMEM((tys,) + bias.shape, F32),
                dma((groups, 5)), dma((groups, FIRST[-1])), dma, dma((2, 2)), dma((txs,)), dma((txs,)), dma((tys,)), dma((tys,)),
                dma((each,)), dma((txs,)), dma((txs,)), dma((txs,)), dma((8, each)), dma((8, each)),
            ],
            compiler_params=pltpu.CompilerParams(collective_id=0, has_side_effects=True, vmem_limit_bytes=60 << 20),
            cost_estimate=pl.CostEstimate(flops=80_000_000_000, bytes_accessed=150_000_000, transcendentals=20_000_000),
            name="encoder",
        )(packed, vec, bias, x_in)
        return out

    return jax.shard_map(local_fn, mesh=mesh, in_specs=in_specs, out_specs=act_spec, check_vma=False)
```

time: 1720 us -> 262 us (0.15)
  the two profiles are of different devices: /device:TPU:97 before, /device:TPU:113 now
where the time goes in v2:
time: 262 us
  Pallas kernels  243 us (93%)
  local copies, waits for them, and re-layouts  17.9 us (7%)
    pallas_call x1, Pallas kernels, local_fn(): pl.pallas_call(functools.partial(kernel, head, each), out_shape=(jax.Shap...  243 us
    unnamed x19, local copies, waits for them, and re-layouts  11.9 us

profile of v2, /device:TPU:113, one launch (start us, length us, event | category | flops | bytes accessed | tf_op | source)
XLA Modules:
  0.0 261.9 jit_solution(4617328155127675367)
XLA Ops:
  0.0 0.0 copy-start
  0.0 0.8 reshape.30
  0.8 0.8 reshape.31
  1.6 0.7 pad_maximum_fusion.1
  2.3 0.7 constant_dynamic-update-slice_fusion.5
  3.0 0.7 constant_dynamic-update-slice_fusion.4
  3.7 0.7 constant_dynamic-update-slice_fusion.3
  4.3 0.7 constant_dynamic-update-slice_fusion.2
  5.0 0.7 constant_dynamic-update-slice_fusion.1
  5.7 0.7 constant_dynamic-update-slice_fusion
  6.4 0.6 pad.8.vec_ref
  7.0 0.6 pad.9.bias_ref
  7.6 0.9 fusion.1
  8.5 0.1 copy.35
  8.7 0.1 copy.36
  8.8 0.0 copy-start.1
  8.8 0.0 copy-start.2
  8.8 0.0 copy-start.3
  8.8 1.3 copy.30
  10.1 0.0 copy-done
  10.2 0.1 copy.37
  10.3 0.1 copy.38
  10.5 0.0 copy-done.1
  10.5 0.0 copy-done.2
  10.5 0.0 copy-done.3
  10.5 0.1 maximum_bitcast_fusion
  10.6 0.2 pad_maximum_fusion
  10.8 1.6 copy.33
  12.3 242.9 %encoder.1 = (bf16[24,576,256]{2,1,0:T(8,128)(2,1)}, bf16[6,8,4,2,2,64,512]{6,5,4,3,2,1,0:T(8,128)(2,1)}) custom-call(bf16[6,2,2,64,512]{4,3,2,1,0:T(8,128)(2,1)} %bitcast.23, f32[16,256]{1,0:T(8,128)} %pad.8.vec_ref, f32[8,896]{1,0:T(8,128)} %pad.9.bias_ref, bf16[24,576,256]{2,1,0:T(8,128)(2,1)} %x_hbm.1), custom_call_target="tpu_custom_call" | custom-call | flops 80000000000 | bytes 150000000 | tf_op jit(solution)/shard_map/encoder/pallas_call | solution.py:413
  255.2 6.7 %copy.45 = bf16[24,576,256]{2,1,0:T(8,128)(2,1)} copy(bf16[24,576,256]{2,1,0:T(8,128)(2,1)} %get-tuple-element.6) | data formatting | bytes 14155776
  (5 shorter events, 0.1 us)
Async XLA Ops:
  0.0 10.1 %copy-start = (bf16[2,512,256]{2,1,0:T(8,128)(2,1)S(1)}, bf16[2,512,256]{2,1,0:T(8,128)(2,1)}, u32[]{:S(2)}) copy-start(bf16[2,512,256]{2,1,0:T(8,128)(2,1)} %param.30) | copy-start | bytes 1572868
  8.8 1.7 copy-start.1
  8.8 1.7 copy-start.2
  8.8 1.7 copy-start.3
